TPU v7x, 32 devices: a whole 2x2x4 slice. The times are simulated.
32 devices in a mesh: sx: 4 (over y, x), sy: 8 (over z, core).
Axes of the slice: x: 2, y: 2, z: 4, core: 2. Of those that a mesh axis runs over, the one named last changes fastest.
Arguments:
- collocation: float32 [2, 4, 2048], P(None, 'sx', 'sy'), may hold values from -1 to 1
- source: float32 [4, 2048], P('sx', 'sy'), may hold values from -31.5 to 40.5
- wall_index: int32 [4, 4, 512], P(None, 'sx', 'sy'), may hold values from 0 to 1023, as said below
- bc_type: int32 [2, 8], P(None, 'sy'), may hold values from 0 to 1
- bc_value: float32 [2, 512], P(None, 'sy'), may hold values from -4 to 4
- in_weight: float32 [4, 3, 4096], P('sx', None, 'sy'), may hold values from -4 to 4
- local_weight: bfloat16 [4, 512, 4096], P('sx', None, 'sy'), may hold values from -0.25 to 0.25
- local_bias: float32 [4, 4096], P('sx', 'sy'), may hold values from -3 to 3
- trunk_weight: bfloat16 [1, 512, 512], replicated, may hold values from -0.25 to 0.25
- trunk_bias: float32 [1, 512], replicated, may hold values from -3 to 3
- head_weight: float32 [4, 4096], P('sx', 'sy'), may hold values from -0.25 to 0.25
Outputs:
- trunk_grad: float32 [1, 512, 512], replicated
- trunk_bias_grad: float32 [1, 512], replicated
- in_grad: float32 [4, 3, 4096], P('sx', None, 'sy')
- local_grad: float32 [4, 512, 4096], P('sx', None, 'sy')
- local_bias_grad: float32 [4, 4096], P('sx', 'sy')
- head_grad: float32 [4, 4096], P('sx', 'sy')
- loss_value: float32 [], replicated
Inputs may be any that keep to these rules, and one draw needn't show every extreme that they name: `wall_index`: within a wall the positions are distinct. A shared wall has the same positions on both sides: wall 0 of (i, j) equals wall 1 of (i - 1, j), and wall 2 of (i, j) equals wall 3 of (i, (j - 1) mod 8).
All inputs are finite; a program needn't handle non-finite values.
Results may differ from a plain program's by a relative error of at most 0.0016.
Values sent between devices are 32-bit elements; how exact they have to be, the bound alone decides.
No kernel may reach another device: no remote copies, remote signals or barrier semaphores. Data moves between devices by JAX's collectives and lax.ppermute only.
A program may use at most 64 MiB of HBM per device.

v0:
```python
import jax
import jax.numpy as jnp
from jax import lax
from jax.sharding import PartitionSpec as P

SLOTS = 1024
HIGH = lax.Precision.HIGHEST
EPS = 1e-06


def extended(x, sides, width, wrap):
    for axis, dim in sides:
        size, length = (lax.axis_size(axis), x.shape[dim])
        up = [(i, (i + 1) % size) for i in range(size if wrap else size - 1)]
        down = [(j, i) for i, j in up]
        last = lax.slice_in_dim(x, length - width, length, axis=dim)
        initial = lax.slice_in_dim(x, 0, width, axis=dim)
        before = lax.ppermute(last, axis, up)
        after = lax.ppermute(initial, axis, down)
        x = jnp.concatenate([before, x, after], axis=dim)
    return x


def activate(preact):
    values = jnp.tanh(preact[0])
    slopes = 1.0 - values * values
    result = [values, slopes * preact[1]]
    if preact.shape[0] == 5:
        curvature = -2.0 * values * slopes
        result.append(slopes * preact[2])
        result.append(slopes * preact[3] + curvature * preact[1] * preact[1])
        result.append(slopes * preact[4] + curvature * preact[2] * preact[2])
    return jnp.stack(result)


def entry_streams(coords, in_weight, directions):
    preact = coords[0][:, None] * in_weight[0] + coords[1][:, None] * in_weight[1] + in_weight[2]
    streams = [preact] + [
        jnp.broadcast_to(2.0 * in_weight[direction], preact.shape) for direction in directions
    ]
    if len(directions) == 2:
        streams = streams + [jnp.zeros_like(preact), jnp.zeros_like(preact)]
    return jnp.stack(streams)


def layer_list(params):
    layers = [(params[1], params[2])]
    layers.append((params[3][0], params[4][0]))
    return layers


def run_forward(coords, directions, params):
    preact = entry_streams(coords, params[0], directions)
    activity, pullback = jax.vjp(activate, preact)
    pullbacks = [pullback]
    lowered = []
    for weight, layer_bias in layer_list(params):
        lowered_in = activity.astype(jnp.bfloat16)
        lowered.append(lowered_in)
        stream_count, row_count, breadth = lowered_in.shape
        product = jnp.dot(
            lowered_in.reshape(stream_count * row_count, breadth),
            weight,
            preferred_element_type=jnp.float32,
        )
        preact = product.reshape(stream_count, row_count, -1)
        preact = preact.at[0].add(layer_bias)
        activity, pullback = jax.vjp(activate, preact)
        pullbacks.append(pullback)
    outputs = jnp.dot(activity, params[5], precision=HIGH)
    return (outputs, (activity, lowered, pullbacks))


def run_backward(coords, directions, params, tape, cotangent):
    activity, lowered, pullbacks = tape
    layers = layer_list(params)
    head_grad = jnp.einsum("kr,krw->w", cotangent, activity, precision=HIGH)
    upstream = cotangent[:, :, None] * params[5]
    weight_grads = []
    bias_grads = []
    for layer_index in reversed(range(len(layers))):
        (preact_grad,) = pullbacks[layer_index + 1](upstream)
        lowered_grad = preact_grad.astype(jnp.bfloat16)
        stream_count, row_count, breadth = lowered_grad.shape
        flat_grad = lowered_grad.reshape(stream_count * row_count, breadth)
        flat_input = lowered[layer_index].reshape(stream_count * row_count, -1)
        weight_grads.insert(
            0,
            lax.dot_general(
                flat_input, flat_grad, (((0,), (0,)), ((), ())), preferred_element_type=jnp.float32
            ),
        )
        bias_grads.insert(0, jnp.sum(preact_grad[0], axis=0))
        upstream = lax.dot_general(
            flat_grad,
            layers[layer_index][0],
            (((1,), (1,)), ((), ())),
            preferred_element_type=jnp.float32,
        ).reshape(stream_count, row_count, -1)
    (entry_grad,) = pullbacks[0](upstream)
    in_grad = jnp.concatenate(
        [jnp.dot(coords, entry_grad[0], precision=HIGH), jnp.sum(entry_grad[0], axis=0)[None]],
        axis=0,
    )
    for stream, direction in enumerate(directions):
        in_grad = in_grad.at[direction].add(2.0 * jnp.sum(entry_grad[1 + stream], axis=0))
    return (
        in_grad,
        weight_grads[0],
        bias_grads[0],
        jnp.stack(weight_grads[1:]),
        jnp.stack(bias_grads[1:]),
        head_grad,
    )


def wall_coords(wall_slots, slot_total):
    spots = (2.0 * wall_slots.astype(jnp.float32) + 1.0) / slot_total - 1.0
    unit_row = jnp.ones_like(spots[0])
    x_coords = jnp.stack(
        [jnp.concatenate([-unit_row, unit_row]), jnp.concatenate([spots[0], spots[1]])]
    )
    y_coords = jnp.stack(
        [jnp.concatenate([spots[2], spots[3]]), jnp.concatenate([-unit_row, unit_row])]
    )
    return (x_coords, y_coords)


def to_rims(outputs):
    half_size = outputs.shape[1] // 2
    return outputs.reshape(2, 2, half_size).transpose(1, 0, 2).reshape(2, 2 * half_size)


def residual_sum(outputs, forcing):
    residual = outputs[3] + outputs[4] + forcing
    return jnp.sum(residual * residual)


def wall_misfit(own_data, neighbour, target, bc_flag, is_outer, normal):
    half_size = own_data.shape[0] // 2
    interface = jnp.sum((own_data - neighbour) ** 2)
    dirichlet = jnp.sum((own_data[:half_size] - target) ** 2)
    neumann = jnp.sum((normal * own_data[half_size:] - target) ** 2)
    boundary = jnp.where(bc_flag == 0, dirichlet, neumann)
    return jnp.where(is_outer, boundary, interface)


def x_misfit(x_rims, neighbours, targets, bc_flags, at_start, at_end):
    return wall_misfit(
        x_rims[0], neighbours[0], targets[0], bc_flags[0], at_start, -1.0
    ) + wall_misfit(x_rims[1], neighbours[1], targets[1], bc_flags[1], at_end, 1.0)


def y_misfit(y_rims, neighbours):
    return jnp.sum((y_rims - neighbours) ** 2)


def blend(inner_grads, wall_grads, inner_factor, wall_factor):
    return tuple(
        (
            inner_factor * inner_part + wall_factor * wall_part
            for inner_part, wall_part in zip(inner_grads, wall_grads)
        )
    )


def per_device(
    collocation,
    source,
    wall_index,
    bc_type,
    bc_value,
    in_weight,
    local_weight,
    local_bias,
    trunk_weight,
    trunk_bias,
    head_weight,
):
    params = (
        in_weight[0],
        local_weight[0],
        local_bias[0],
        trunk_weight,
        trunk_bias,
        head_weight[0],
    )
    points = collocation[:, 0, :]
    forcing = source[0]
    x_coords, y_coords = wall_coords(wall_index[:, 0, :], SLOTS)
    x_out, x_tape = run_forward(x_coords, (0,), params)
    y_out, y_tape = run_forward(y_coords, (1,), params)
    x_rims = to_rims(x_out)
    y_rims = to_rims(y_out)
    x_padded = extended(x_rims, (("sx", 0),), 1, False)
    y_padded = extended(y_rims, (("sy", 0),), 1, True)
    inner_out, inner_tape = run_forward(points, (0, 1), params)
    residual_total, inner_cotangent = jax.value_and_grad(residual_sum)(inner_out, forcing)
    row_place = lax.axis_index("sx")
    at_start = row_place == 0
    at_end = row_place == lax.axis_size("sx") - 1
    x_total, x_rim_grad = jax.value_and_grad(x_misfit)(
        x_rims, jnp.stack([x_padded[0], x_padded[3]]), bc_value, bc_type[:, 0], at_start, at_end
    )
    y_total, y_rim_grad = jax.value_and_grad(y_misfit)(
        y_rims, jnp.stack([y_padded[0], y_padded[3]])
    )
    wall_total = x_total + y_total
    inner_grads = run_backward(points, (0, 1), params, inner_tape, inner_cotangent)
    x_grads = run_backward(x_coords, (0,), params, x_tape, to_rims(x_rim_grad))
    y_grads = run_backward(y_coords, (1,), params, y_tape, to_rims(y_rim_grad))
    wall_grads = tuple(
        (first_part + second_part for first_part, second_part in zip(x_grads, y_grads))
    )
    devices_all = lax.axis_size("sx") * lax.axis_size("sy")
    inner_count = points.shape[1] * devices_all
    wall_count = 4 * wall_index.shape[2] * devices_all
    gathered = lax.psum(
        (residual_total, wall_total, inner_grads[3], inner_grads[4], wall_grads[3], wall_grads[4]),
        ("sx", "sy"),
    )
    inner_mean = gathered[0] / inner_count
    wall_mean = gathered[1] / wall_count
    balance_weight = jnp.sqrt((wall_mean + EPS) / (inner_mean + EPS))
    combined = blend(inner_grads, wall_grads, balance_weight / inner_count, 1.0 / wall_count)
    trunk_grad, trunk_bias_grad = blend(
        (gathered[2], gathered[3]),
        (gathered[4], gathered[5]),
        balance_weight / inner_count,
        1.0 / wall_count,
    )
    loss_value = balance_weight * inner_mean + wall_mean
    return (
        trunk_grad,
        trunk_bias_grad,
        combined[0][None],
        combined[1][None],
        combined[2][None],
        combined[5][None],
        loss_value,
    )


def solution(mesh):
    return jax.shard_map(
        per_device,
        mesh=mesh,
        in_specs=(
            P(None, "sx", "sy"),
            P("sx", "sy"),
            P(None, "sx", "sy"),
            P(None, "sy"),
            P(None, "sy"),
            P("sx", None, "sy"),
            P("sx", None, "sy"),
            P("sx", "sy"),
            P(),
            P(),
            P("sx", "sy"),
        ),
        out_specs=(
            P(),
            P(),
            P("sx", None, "sy"),
            P("sx", None, "sy"),
            P("sx", "sy"),
            P("sx", "sy"),
            P(),
        ),
        check_vma=False,
    )
```

profile of v0, /device:TPU:0, one launch (start us, length us, event | category | flops | bytes accessed | tf_op | source)
XLA Modules:
  0.0 322.9 jit_solution(16296578300917998260)
XLA Ops:
  9.7 1.5 fusion.68
  11.2 1.3 fusion.66
  19.8 1.3 slice.443
  21.2 6.0 %collective-permute-start = (f32[1,128]{1,0:T(1,128)}, f32[1,128]{1,0:T(1,128)}, u32[]{:S(2)}, u32[]{:S(2)}) collective-permute-start(f32[1,128]{1,0:T(1,128)} %slice.443), channel_id=1, source_target_pairs={{0,8},{8,16},{16,24},{1,9},{9,17},{17,25},{2,10},{10,18},{18,26},{... | collective-permute-start | bytes 1544 | tf_op jit(solution)/shard_map/ppermute | solution.py:18
  27.2 1.4 fusion.26
  31.0 3.0 collective-permute-start.3
  34.0 1.3 slice.458
  48.5 2.3 fusion.150
  53.8 2.0 fusion.190
  55.8 1.9 convolution_bitcast_fusion.5
  60.0 1.9 fusion.188
  66.2 3.7 %fusion.145 = f32[1,512,1]{1,0,2:T(1,128)} fusion(f32[5,256,512]{2,1,0:T(8,128)} %copy-done.2, f32[5,256,1]{1,0,2:T(8,128)} %get-tuple-element.247), kind=kOutput, calls=%fused_computation.294 | convolution fusion | flops 7864320 | bytes 2628608 | tf_op jit(solution)/shard_map/kr,krw->w/dot_general | solution.py:77
  69.9 1.7 slice_reduce_fusion.3
  71.6 1.6 slice_reduce_fusion
  77.6 2.0 multiply_reduce_fusion.4
  82.3 1.3 scatter-add.15
  85.7 1.3 reshape.1820
  89.6 1.3 mul.1249
  91.4 1.7 reduce.49
  94.5 1.8 reduce.50
  99.4 1.3 reshape.1855
  100.7 1.3 mul.1260
  110.3 1.8 reduce.52
  113.4 1.8 reduce.51
  120.3 39.4 %all-reduce.47 = (f32[]{:T(128)}, f32[]{:T(128)}, f32[1,512]{1,0:T(1,128)}, f32[1,512]{1,0:T(1,128)}) all-reduce(f32[]{:T(128)S(6)} %add.491, f32[]{:T(128)} %get-tuple-element.162, f32[1,512]{1,0:T(1,128)S(1)} %bitcast.531, f32[1,512]{1,0:T(1,128)} %bitcast.529), channel_id=1, replica_groups=mesh['sx'=4,'sy'=8] {'sx','sy'}, use_global_device_ids=true, to_apply=%region_7.0 | all-reduce | flops 1026 | bytes 8208 | tf_op jit(solution)/shard_map/psum | solution.py:218
  161.2 2.0 fusion.30
  163.2 1.9 fusion.34
  166.4 2.4 convolution_bitcast_fusion
  180.6 1.6 fusion.6
  182.2 1.8 fusion.2
  184.0 128.1 %all-reduce.51.cloned.1.call-done = (f32[1,512,512]{2,1,0:T(8,128)}, f32[1,512,512]{2,1,0:T(8,128)}) async-done(((f32[1,512,512]{2,1,0:T(8,128)}, f32[1,512,512]{2,1,0:T(8,128)}), (f32[1,512,512]{2,1,0:T(8,128)}, f32[1,512,512]{2,1,0:T(8,128)})) %all-reduce.51.cloned.1.call-update) | async-done | bytes 2097168 | tf_op jit(solution)/shard_map/psum | solution.py:218
  312.2 2.7 multiply_add_fusion
  (229 shorter events, 72.8 us)
Async XLA Ops:
  7.2 5.6 %copy-start = (bf16[1,512,512]{2,1,0:T(8,128)(2,1)S(1)}, bf16[1,512,512]{2,1,0:T(8,128)(2,1)}, u32[]{:S(2)}) copy-start(bf16[1,512,512]{2,1,0:T(8,128)(2,1)} %param.39) | copy-start | bytes 1572868
  7.2 5.4 %copy-start.28 = (f32[1,512]{1,0:T(1,128)S(1)}, f32[1,512]{1,0:T(1,128)}, u32[]{:S(2)}) copy-start(f32[1,512]{1,0:T(1,128)} %param.38) | copy-start | bytes 6148
  7.2 305.0 %all-reduce.51.cloned.1.call-start = ((), (), s32[]{:S(2)}) async-start(), calls=%async_computation | async-start | bytes 4194304 | tf_op jit(solution)/shard_map/psum | solution.py:218
  8.7 3.8 %copy-start.31 = (f32[512]{0:T(512)}, f32[512]{0:T(512)S(1)}, u32[]{:S(2)}) copy-start(f32[512]{0:T(512)S(1)} %get-tuple-element.253) | copy-start | bytes 6148
  8.7 3.8 %copy-start.34 = (f32[512]{0:T(512)}, f32[512]{0:T(512)S(1)}, u32[]{:S(2)}) copy-start(f32[512]{0:T(512)S(1)} %get-tuple-element.254) | copy-start | bytes 6148
  8.8 3.8 %copy-start.48 = (f32[128]{0:T(128)}, f32[128]{0:T(128)S(1)}, u32[]{:S(2)}) copy-start(f32[128]{0:T(128)S(1)} %get-tuple-element.251) | copy-start | bytes 1540
  8.8 3.8 %copy-start.50 = (f32[128]{0:T(128)}, f32[128]{0:T(128)S(1)}, u32[]{:S(2)}) copy-start(f32[128]{0:T(128)S(1)} %get-tuple-element.252) | copy-start | bytes 1540
  9.7 3.4 %copy-start.17 = (bf16[1,128,512]{2,1,0:T(8,128)(2,1)}, bf16[1,128,512]{2,1,0:T(8,128)(2,1)S(1)}, u32[]{:S(2)}) copy-start(bf16[1,128,512]{2,1,0:T(8,128)(2,1)S(1)} %get-tuple-element.215) | copy-start | bytes 393220
  13.1 30.0 %copy-start.6 = (f32[2,128,512]{2,1,0:T(8,128)}, f32[2,128,512]{2,1,0:T(8,128)S(1)}, u32[]{:S(2)}) copy-start(f32[2,128,512]{2,1,0:T(8,128)S(1)} %fusion.56) | copy-start | bytes 1572868
  13.7 31.3 %copy-start.1 = (bf16[1,512,512]{2,1,0:T(8,128)(2,1)S(1)}, bf16[1,512,512]{2,1,0:T(8,128)(2,1)}, u32[]{:S(2)}) copy-start(bf16[1,512,512]{2,1,0:T(8,128)(2,1)} %param.37) | copy-start | bytes 1572868
  14.7 31.2 %copy-start.3 = (f32[1,128,512]{2,1,0:T(8,128)}, f32[1,128,512]{2,1,0:T(8,128)S(1)}, u32[]{:S(2)}) copy-start(f32[1,128,512]{2,1,0:T(8,128)S(1)} %get-tuple-element.238) | copy-start | bytes 786436
  14.7 31.2 %copy-start.4 = (f32[1,128,512]{2,1,0:T(8,128)}, f32[1,128,512]{2,1,0:T(8,128)S(1)}, u32[]{:S(2)}) copy-start(f32[1,128,512]{2,1,0:T(8,128)S(1)} %get-tuple-element.169) | copy-start | bytes 786436
  14.7 31.2 %copy-start.12 = (f32[1,128,512]{2,1,0:T(8,128)}, f32[1,128,512]{2,1,0:T(8,128)S(1)}, u32[]{:S(2)}) copy-start(f32[1,128,512]{2,1,0:T(8,128)S(1)} %get-tuple-element.237) | copy-start | bytes 786436
  18.6 65.0 %collective-permute-start.1 = (f32[1,128]{1,0:T(1,128)}, f32[1,128]{1,0:T(1,128)}, u32[]{:S(2)}, u32[]{:S(2)}) collective-permute-start(f32[1,128]{1,0:T(1,128)} %slice.450), channel_id=1, source_target_pairs={{8,0},{16,8},{24,16},{9,1},{17,9},{25,17},{10,2},{18,10},{26,18},{... | collective-permute-start | bytes 1544 | tf_op jit(solution)/shard_map/ppermute | solution.py:19
  21.2 63.2 %collective-permute-start = (f32[1,128]{1,0:T(1,128)}, f32[1,128]{1,0:T(1,128)}, u32[]{:S(2)}, u32[]{:S(2)}) collective-permute-start(f32[1,128]{1,0:T(1,128)} %slice.443), channel_id=1, source_target_pairs={{0,8},{8,16},{16,24},{1,9},{9,17},{17,25},{2,10},{10,18},{18,26},{... | collective-permute-start | bytes 1544 | tf_op jit(solution)/shard_map/ppermute | solution.py:18
  31.0 59.9 %collective-permute-start.3 = (f32[1,128]{1,0:T(1,128)}, f32[1,128]{1,0:T(1,128)}, u32[]{:S(2)}, u32[]{:S(2)}) collective-permute-start(f32[1,128]{1,0:T(1,128)} %slice.460), channel_id=1, source_target_pairs={{1,0},{2,1},{3,2},{4,3},{5,4},{6,5},{7,6},{0,7},{9,8},{10,9},{11,1... | collective-permute-start | bytes 1544 | tf_op jit(solution)/shard_map/ppermute | solution.py:19
  35.3 59.2 %collective-permute-start.2 = (f32[1,128]{1,0:T(1,128)}, f32[1,128]{1,0:T(1,128)}, u32[]{:S(2)}, u32[]{:S(2)}) collective-permute-start(f32[1,128]{1,0:T(1,128)} %slice.458), channel_id=1, source_target_pairs={{0,1},{1,2},{2,3},{3,4},{4,5},{5,6},{6,7},{7,0},{8,9},{9,10},{10,1... | collective-permute-start | bytes 1544 | tf_op jit(solution)/shard_map/ppermute | solution.py:18
  48.5 3.6 %copy-start.2 = (f32[5,256,512]{2,1,0:T(8,128)}, f32[5,256,512]{2,1,0:T(8,128)S(1)}, u32[]{:S(2)}) copy-start(f32[5,256,512]{2,1,0:T(8,128)S(1)} %add_dynamic-update-slice_fusion) | copy-start | bytes 7864324
  66.2 7.0 %copy-start.47 = (f32[512]{0:T(512)S(1)}, f32[512]{0:T(512)}, u32[]{:S(2)}) copy-start(f32[512]{0:T(512)} %get-tuple-element.141) | copy-start | bytes 6148
  66.2 7.6 %copy-start.46 = (f32[512]{0:T(512)S(1)}, f32[512]{0:T(512)}, u32[]{:S(2)}) copy-start(f32[512]{0:T(512)} %get-tuple-element.143) | copy-start | bytes 6148
  66.2 7.6 %copy-start.42 = (f32[2,512]{1,0:T(2,128)S(1)}, f32[2,512]{1,0:T(2,128)}, u32[]{:S(2)}) copy-start(f32[2,512]{1,0:T(2,128)} %convolution_bitcast_fusion.6) | copy-start | bytes 12292
  66.2 8.2 %copy-start.44 = (f32[512]{0:T(512)S(1)}, f32[512]{0:T(512)}, u32[]{:S(2)}) copy-start(f32[512]{0:T(512)} %get-tuple-element.142) | copy-start | bytes 6148
  107.3 9.2 %copy-start.41 = (f32[1,2,2,64]{3,1,2,0:T(2,128)S(1)}, f32[1,2,2,64]{3,1,2,0:T(2,128)}, u32[]{:S(2)}) copy-start(f32[1,2,2,64]{3,1,2,0:T(2,128)} %copy-done.40) | copy-start | bytes 3076
  161.1 7.7 %copy-start.14 = (bf16[2,128,512]{2,1,0:T(8,128)(2,1)S(1)}, bf16[2,128,512]{2,1,0:T(8,128)(2,1)}, u32[]{:S(2)}) copy-start(bf16[2,128,512]{2,1,0:T(8,128)(2,1)} %fusion.10) | copy-start | bytes 786436
  161.1 8.0 %copy-start.33 = (f32[512]{0:T(512)S(1)}, f32[512]{0:T(512)}, u32[]{:S(2)}) copy-start(f32[512]{0:T(512)} %copy-done.31) | copy-start | bytes 6148
  161.1 8.0 %copy-start.36 = (f32[512]{0:T(512)S(1)}, f32[512]{0:T(512)}, u32[]{:S(2)}) copy-start(f32[512]{0:T(512)} %copy-done.34) | copy-start | bytes 6148
  161.1 8.0 %copy-start.49 = (f32[128]{0:T(128)S(1)}, f32[128]{0:T(128)}, u32[]{:S(2)}) copy-start(f32[128]{0:T(128)} %copy-done.48) | copy-start | bytes 1540
  161.1 8.0 %copy-start.51 = (f32[128]{0:T(128)S(1)}, f32[128]{0:T(128)}, u32[]{:S(2)}) copy-start(f32[128]{0:T(128)} %copy-done.50) | copy-start | bytes 1540
  161.2 8.0 %copy-start.52 = (f32[128]{0:T(128)S(1)}, f32[128]{0:T(128)}, u32[]{:S(2)}) copy-start(f32[128]{0:T(128)} %constant.271.clone.1) | copy-start | bytes 1540
  169.6 5.8 %copy-start.39 = (f32[3,512]{1,0:T(4,128)S(1)}, f32[3,512]{1,0:T(4,128)}, u32[]{:S(2)}) copy-start(f32[3,512]{1,0:T(4,128)} %scatter-add.15) | copy-start | bytes 18436
  170.5 10.0 %copy-start.9 = (bf16[2,128,512]{2,1,0:T(8,128)(2,1)S(1)}, bf16[2,128,512]{2,1,0:T(8,128)(2,1)}, u32[]{:S(2)}) copy-start(bf16[2,128,512]{2,1,0:T(8,128)(2,1)} %fusion.9) | copy-start | bytes 786436
  173.3 8.9 %copy-start.16 = (bf16[5,256,512]{2,1,0:T(8,128)(2,1)S(1)}, bf16[5,256,512]{2,1,0:T(8,128)(2,1)}, u32[]{:S(2)}) copy-start(bf16[5,256,512]{2,1,0:T(8,128)(2,1)} %copy-done.15) | copy-start | bytes 3932164
  (28 other events, 52.1 us)
Sparse Core Ops, SparseCore 0:
  176.9 135.2 all-reduce.50
where the time goes:
time: 325 us; the launch traced here: 323 us
  waiting for transfers between devices  128 us (39%)
  other arithmetic  54.6 us (17%)
  blocking collectives  39.4 us (12%)
  local copies, waits for them, and re-layouts  35.2 us (11%)
  matrix products  31.9 us (10%)
  between operations  23.3 us (7%)
  starting transfers between devices  10.3 us (3%)
    psum x1, waiting for transfers between devices, per_device(): lax.psum((residual_total, wall_total, inner_grads[3], inner_grads[4], wal...  128 us
    psum x1, blocking collectives, per_device(): lax.psum((residual_total, wall_total, inner_grads[3], inner_grads[4], wal...  39.4 us
    dot_general x6, matrix products, run_backward(): lax.dot_general(flat_input, flat_grad, (((0,), (0,)), ((), ())), preferre...  9.33 us
    dot_general x3, matrix products, run_backward(): head_grad = jnp.einsum('kr,krw->w', cotangent, activity, precision=HIGH)  7.62 us
    add x4, other arithmetic, blend(): inner_factor * inner_part + wall_factor * wall_part  6.55 us
  transfers between devices with their start and end apart: 5, of which 1 were waited for; matrix products, arithmetic and copies ran while one was open for 21% of the time, Pallas kernels for 0%

commit v1 on v0

--- a/solution.py
+++ b/solution.py
@@ -215,10 +215,11 @@
     devices_all = lax.axis_size("sx") * lax.axis_size("sy")
     inner_count = points.shape[1] * devices_all
     wall_count = 4 * wall_index.shape[2] * devices_all
-    gathered = lax.psum(
+    inner = lax.psum(
         (residual_total, wall_total, inner_grads[3], inner_grads[4], wall_grads[3], wall_grads[4]),
-        ("sx", "sy"),
-    )
+        "sy",
+    )
+    gathered = lax.psum(inner, "sx")
     inner_mean = gathered[0] / inner_count
     wall_mean = gathered[1] / wall_count
     balance_weight = jnp.sqrt((wall_mean + EPS) / (inner_mean + EPS))

time: 325 us -> 254 us (0.78)
  waiting for transfers between devices: 128 us -> 88.5 us
  blocking collectives: 39.4 us -> 28.6 us
  local copies, waits for them, and re-layouts: 35.2 us -> 25.7 us
  other arithmetic: 54.6 us -> 49 us
  matrix products: 31.9 us -> 26.8 us
    psum x1, waiting for transfers between devices: 128 us -> 26.4 us  [per_device(): lax.psum((residual_total, wall_total, inner_grads[3], inner_grads[4], wal...]
    psum x0 -> x1, waiting for transfers between devices: none -> 62 us  [per_device(): gathered = lax.psum(inner, 'sx')]
    psum x1, blocking collectives: 39.4 us -> 18.6 us  [per_device(): lax.psum((residual_total, wall_total, inner_grads[3], inner_grads[4], wal...]
    psum x0 -> x1, blocking collectives: none -> 10 us  [per_device(): gathered = lax.psum(inner, 'sx')]
  transfers between devices with their start and end apart: 5 -> 6, of which waited for: 1 -> 2; matrix products, arithmetic and copies ran while one was open for 21% -> 29% of each run, Pallas kernels for 0% -> 0%
where the time goes in v1:
time: 254 us; the launch traced here: 252 us
  waiting for transfers between devices  88.5 us (35%)
  other arithmetic  49 us (19%)
  blocking collectives  28.6 us (11%)
  matrix products  26.8 us (11%)
  local copies, waits for them, and re-layouts  25.7 us (10%)
  between operations  23.5 us (9%)
  starting transfers between devices  10.4 us (4%)
    psum x1, waiting for transfers between devices, per_device(): gathered = lax.psum(inner, 'sx')  62 us
    psum x1, waiting for transfers between devices, per_device(): lax.psum((residual_total, wall_total, inner_grads[3], inner_grads[4], wal...  26.4 us
    psum x1, blocking collectives, per_device(): lax.psum((residual_total, wall_total, inner_grads[3], inner_grads[4], wal...  18.6 us
    psum x1, blocking collectives, per_device(): gathered = lax.psum(inner, 'sx')  10 us
    reduce_sum x6, other arithmetic, run_backward(): bias_grads.insert(0, jnp.sum(preact_grad[0], axis=0))  7.3 us
    dot_general x6, matrix products, run_backward(): lax.dot_general(flat_input, flat_grad, (((0,), (0,)), ((), ())), preferre...  7 us
    ppermute x2, starting transfers between devices, extended(): before = lax.ppermute(last, axis, up)  6.01 us
    mul x4, local copies, waits for them, and re-layouts, run_backward(): upstream = cotangent[:, :, None] * params[5]  5.33 us
  transfers between devices with their start and end apart: 6, of which 2 were waited for; matrix products, arithmetic and copies ran while one was open for 29% of the time, Pallas kernels for 0%

profile of v1, /device:TPU:0, one launch (start us, length us, event | category | flops | bytes accessed | tf_op | source)
XLA Modules:
  0.0 252.3 jit_solution(4866765783376346382)
XLA Ops:
  9.7 1.5 fusion.68
  11.2 1.3 fusion.66
  18.3 6.0 %collective-permute-start = (f32[1,128]{1,0:T(1,128)}, f32[1,128]{1,0:T(1,128)}, u32[]{:S(2)}, u32[]{:S(2)}) collective-permute-start(f32[1,128]{1,0:T(1,128)} %slice.443), channel_id=1, source_target_pairs={{0,8},{8,16},{16,24},{1,9},{9,17},{17,25},{2,10},{10,18},{18,26},{... | collective-permute-start | bytes 1544 | tf_op jit(solution)/shard_map/ppermute | solution.py:18
  25.7 3.0 %collective-permute-start.3 = (f32[1,128]{1,0:T(1,128)}, f32[1,128]{1,0:T(1,128)}, u32[]{:S(2)}, u32[]{:S(2)}) collective-permute-start(f32[1,128]{1,0:T(1,128)} %slice.460), channel_id=1, source_target_pairs={{1,0},{2,1},{3,2},{4,3},{5,4},{6,5},{7,6},{0,7},{9,8},{10,9},{11,1... | collective-permute-start | bytes 1544 | tf_op jit(solution)/shard_map/ppermute | solution.py:19
  37.0 2.3 fusion.150
  42.3 2.1 fusion.190
  44.3 1.8 convolution_bitcast_fusion.5
  48.4 1.8 fusion.188
  54.7 3.7 %fusion.145 = f32[1,512,1]{1,0,2:T(1,128)} fusion(f32[5,256,512]{2,1,0:T(8,128)} %copy-done.2, f32[5,256,1]{1,0,2:T(8,128)} %get-tuple-element.253), kind=kOutput, calls=%fused_computation.294 | convolution fusion | flops 7864320 | bytes 2628608 | tf_op jit(solution)/shard_map/kr,krw->w/dot_general | solution.py:77
  58.4 1.7 slice_reduce_fusion.3
  60.1 1.7 slice_reduce_fusion
  63.5 1.3 scatter-add.14
  66.1 2.0 multiply_reduce_fusion.4
  70.7 1.3 scatter-add.15
  74.7 1.7 reduce.52
  77.7 1.8 reduce.51
  80.8 1.3 reshape.1820
  83.4 1.3 mul.1249
  84.7 1.8 reduce.49
  87.8 1.8 reduce.50
  89.7 1.3 stack.111
  91.0 1.3 multiply_reduce_fusion
  92.9 1.3 mul.1260
  108.0 18.6 %all-reduce.47 = (f32[]{:T(128)}, f32[]{:T(128)}, f32[1,512]{1,0:T(1,128)S(1)}, f32[1,512]{1,0:T(1,128)S(1)}) all-reduce(f32[]{:T(128)S(6)} %add.503, f32[]{:T(128)} %get-tuple-element.168, f32[1,512]{1,0:T(1,128)S(1)} %bitcast.532, f32[1,512]{1,0:T(1,128)} %bitcast.529), channel_id=1, replica_groups=mesh['sx'=4,'sy'=8] {'sy'}, use_global_device_ids=true, to_apply=%region_7.0 | all-reduce | flops 1026 | bytes 8208 | tf_op jit(solution)/shard_map/psum | solution.py:218
  126.6 10.0 %all-reduce.49 = (f32[]{:T(128)}, f32[]{:T(128)}, f32[1,512]{1,0:T(1,128)}, f32[1,512]{1,0:T(1,128)}) all-reduce(f32[]{:T(128)} %get-tuple-element.154, f32[]{:T(128)} %get-tuple-element.155, f32[1,512]{1,0:T(1,128)S(1)} %get-tuple-element.156, f32[1,512]{1,0:T(1,128)S(1)} %get-tuple-element.157), channel_id=1, replica_groups=mesh['sx'=4,'sy'=8] {'sx'}, use_global_device_ids=true, to_apply=%region_8.0 | all-reduce | flops 1026 | bytes 8208 | tf_op jit(solution)/shard_map/psum | solution.py:222
  136.6 1.3 reshape.1853
  137.9 1.3 reshape.1855
  142.9 26.4 %all-reduce.54.cloned.1.call-done = (f32[1,512,512]{2,1,0:T(8,128)}, f32[1,512,512]{2,1,0:T(8,128)}) async-done(((f32[1,512,512]{2,1,0:T(8,128)}, f32[1,512,512]{2,1,0:T(8,128)}), (f32[1,512,512]{2,1,0:T(8,128)}, f32[1,512,512]{2,1,0:T(8,128)})) %all-reduce.54.cloned.1.call-update) | async-done | bytes 2097168 | tf_op jit(solution)/shard_map/psum | solution.py:218
  172.9 1.4 convolution_bitcast_fusion
  177.8 1.8 fusion.2
  179.7 62.0 %all-reduce.56.cloned.1.call-done = (f32[1,512,512]{2,1,0:T(8,128)}, f32[1,512,512]{2,1,0:T(8,128)}) async-done(((f32[1,512,512]{2,1,0:T(8,128)}, f32[1,512,512]{2,1,0:T(8,128)}), (f32[1,512,512]{2,1,0:T(8,128)}, f32[1,512,512]{2,1,0:T(8,128)})) %all-reduce.56.cloned.1.call-update) | async-done | bytes 2097168 | tf_op jit(solution)/shard_map/psum | solution.py:222
  241.6 2.7 %multiply_add_fusion = f32[1,512,512]{2,1,0:T(8,128)} fusion(f32[1,512,512]{2,1,0:T(8,128)} %get-tuple-element.164, f32[1,512,512]{2,1,0:T(8,128)} %get-tuple-element.165, f32[]{:T(128)S(6)} %div.27), kind=kLoop, calls=%fused_computation.18 | loop fusion | flops 786432 | bytes 3145732 | tf_op jit(solution)/shard_map/add | solution.py:161
  (273 shorter events, 57.9 us)
Async XLA Ops:
  7.2 5.6 %copy-start = (bf16[1,512,512]{2,1,0:T(8,128)(2,1)S(1)}, bf16[1,512,512]{2,1,0:T(8,128)(2,1)}, u32[]{:S(2)}) copy-start(bf16[1,512,512]{2,1,0:T(8,128)(2,1)} %param.39) | copy-start | bytes 1572868
  7.2 162.2 %all-reduce.54.cloned.1.call-start = ((), (), s32[]{:S(2)}) async-start(), calls=%async_computation | async-start | bytes 4194304 | tf_op jit(solution)/shard_map/psum | solution.py:218
  8.7 24.3 %copy-start.45 = (f32[512]{0:T(512)}, f32[512]{0:T(512)S(1)}, u32[]{:S(2)}) copy-start(f32[512]{0:T(512)S(1)} %get-tuple-element.260) | copy-start | bytes 6148
  8.7 24.6 %copy-start.42 = (f32[512]{0:T(512)}, f32[512]{0:T(512)S(1)}, u32[]{:S(2)}) copy-start(f32[512]{0:T(512)S(1)} %get-tuple-element.259) | copy-start | bytes 6148
  12.8 16.6 %copy-start.71 = (s32[2,1]{0,1:T(1,128)S(1)}, s32[2,1]{0,1:T(1,128)}, u32[]{:S(2)}) copy-start(s32[2,1]{0,1:T(1,128)} %param.34) | copy-start | bytes 28
  12.8 19.6 %copy-start.57 = (f32[2,1,256]{2,1,0:T(1,128)S(1)}, f32[2,1,256]{2,1,0:T(1,128)}, u32[]{:S(2)}) copy-start(f32[2,1,256]{2,1,0:T(1,128)} %param.31) | copy-start | bytes 6148
  13.7 20.0 %copy-start.1 = (bf16[1,512,512]{2,1,0:T(8,128)(2,1)S(1)}, bf16[1,512,512]{2,1,0:T(8,128)(2,1)}, u32[]{:S(2)}) copy-start(bf16[1,512,512]{2,1,0:T(8,128)(2,1)} %param.37) | copy-start | bytes 1572868
  13.9 20.6 %copy-start.3 = (f32[1,128,512]{2,1,0:T(8,128)}, f32[1,128,512]{2,1,0:T(8,128)S(1)}, u32[]{:S(2)}) copy-start(f32[1,128,512]{2,1,0:T(8,128)S(1)} %get-tuple-element.244) | copy-start | bytes 786436
  13.9 20.6 %copy-start.13 = (f32[1,128,512]{2,1,0:T(8,128)}, f32[1,128,512]{2,1,0:T(8,128)S(1)}, u32[]{:S(2)}) copy-start(f32[1,128,512]{2,1,0:T(8,128)S(1)} %get-tuple-element.243) | copy-start | bytes 786436
  16.5 55.6 %collective-permute-start.1 = (f32[1,128]{1,0:T(1,128)}, f32[1,128]{1,0:T(1,128)}, u32[]{:S(2)}, u32[]{:S(2)}) collective-permute-start(f32[1,128]{1,0:T(1,128)} %slice.450), channel_id=1, source_target_pairs={{8,0},{16,8},{24,16},{9,1},{17,9},{25,17},{10,2},{18,10},{26,18},{... | collective-permute-start | bytes 1544 | tf_op jit(solution)/shard_map/ppermute | solution.py:19
  18.3 54.5 %collective-permute-start = (f32[1,128]{1,0:T(1,128)}, f32[1,128]{1,0:T(1,128)}, u32[]{:S(2)}, u32[]{:S(2)}) collective-permute-start(f32[1,128]{1,0:T(1,128)} %slice.443), channel_id=1, source_target_pairs={{0,8},{8,16},{16,24},{1,9},{9,17},{17,25},{2,10},{10,18},{18,26},{... | collective-permute-start | bytes 1544 | tf_op jit(solution)/shard_map/ppermute | solution.py:18
  25.1 9.5 %copy-start.54 = (f32[1,2,2,64]{3,0,2,1:T(1,128)}, f32[1,2,2,64]{3,0,2,1:T(1,128)S(1)}, u32[]{:S(2)}) copy-start(f32[1,2,2,64]{3,0,2,1:T(1,128)S(1)} %fusion.26) | copy-start | bytes 3076
  25.7 59.0 %collective-permute-start.3 = (f32[1,128]{1,0:T(1,128)}, f32[1,128]{1,0:T(1,128)}, u32[]{:S(2)}, u32[]{:S(2)}) collective-permute-start(f32[1,128]{1,0:T(1,128)} %slice.460), channel_id=1, source_target_pairs={{1,0},{2,1},{3,2},{4,3},{5,4},{6,5},{7,6},{0,7},{9,8},{10,9},{11,1... | collective-permute-start | bytes 1544 | tf_op jit(solution)/shard_map/ppermute | solution.py:19
  29.3 58.5 %collective-permute-start.2 = (f32[1,128]{1,0:T(1,128)}, f32[1,128]{1,0:T(1,128)}, u32[]{:S(2)}, u32[]{:S(2)}) collective-permute-start(f32[1,128]{1,0:T(1,128)} %slice.458), channel_id=1, source_target_pairs={{0,1},{1,2},{2,3},{3,4},{4,5},{5,6},{6,7},{7,0},{8,9},{9,10},{10,1... | collective-permute-start | bytes 1544 | tf_op jit(solution)/shard_map/ppermute | solution.py:18
  54.7 7.1 %copy-start.60 = (f32[512]{0:T(512)S(1)}, f32[512]{0:T(512)}, u32[]{:S(2)}) copy-start(f32[512]{0:T(512)} %get-tuple-element.141) | copy-start | bytes 6148
  54.7 7.7 %copy-start.59 = (f32[512]{0:T(512)S(1)}, f32[512]{0:T(512)}, u32[]{:S(2)}) copy-start(f32[512]{0:T(512)} %get-tuple-element.143) | copy-start | bytes 6148
  54.7 7.7 %copy-start.53 = (f32[2,512]{1,0:T(2,128)S(1)}, f32[2,512]{1,0:T(2,128)}, u32[]{:S(2)}) copy-start(f32[2,512]{1,0:T(2,128)} %convolution_bitcast_fusion.6) | copy-start | bytes 12292
  54.7 8.3 %copy-start.56 = (f32[512]{0:T(512)S(1)}, f32[512]{0:T(512)}, u32[]{:S(2)}) copy-start(f32[512]{0:T(512)} %get-tuple-element.142) | copy-start | bytes 6148
  103.1 38.1 %copy-start.61 = (f32[512]{0:T(512)S(1)}, f32[512]{0:T(512)}, u32[]{:S(2)}) copy-start(f32[512]{0:T(512)} %broadcast_multiply_fusion.3) | copy-start | bytes 6148
  103.2 66.2 %copy-start.49 = (f32[3,512]{1,0:T(4,128)S(1)}, f32[3,512]{1,0:T(4,128)}, u32[]{:S(2)}) copy-start(f32[3,512]{1,0:T(4,128)} %scatter-add.15) | copy-start | bytes 18436
  103.2 138.5 %all-reduce.56.cloned.1.call-start = ((), (), s32[]{:S(2)}) async-start(), calls=%async_computation.1 | async-start | bytes 4194304 | tf_op jit(solution)/shard_map/psum | solution.py:222
  141.9 32.4 %copy-start.7 = (f32[1,128,512]{2,1,0:T(8,128)S(1)}, f32[1,128,512]{2,1,0:T(8,128)}, u32[]{:S(2)}) copy-start(f32[1,128,512]{2,1,0:T(8,128)} %copy-done.5) | copy-start | bytes 786436
  141.9 32.4 %copy-start.16 = (f32[1,128,512]{2,1,0:T(8,128)S(1)}, f32[1,128,512]{2,1,0:T(8,128)}, u32[]{:S(2)}) copy-start(f32[1,128,512]{2,1,0:T(8,128)} %copy-done.15) | copy-start | bytes 786436
  169.4 5.9 %copy-start.4 = (f32[1,128,512]{2,1,0:T(8,128)S(1)}, f32[1,128,512]{2,1,0:T(8,128)}, u32[]{:S(2)}) copy-start(f32[1,128,512]{2,1,0:T(8,128)} %copy-done.3) | copy-start | bytes 786436
  169.4 5.9 %copy-start.14 = (f32[1,128,512]{2,1,0:T(8,128)S(1)}, f32[1,128,512]{2,1,0:T(8,128)}, u32[]{:S(2)}) copy-start(f32[1,128,512]{2,1,0:T(8,128)} %copy-done.13) | copy-start | bytes 786436
  169.4 5.9 %copy-start.67 = (f32[2,128,1]{1,0,2:T(2,128)S(1)}, f32[2,128,1]{1,0,2:T(2,128)}, u32[]{:S(2)}) copy-start(f32[2,128,1]{1,0,2:T(2,128)} %reshape.1855) | copy-start | bytes 3076
  169.4 6.3 %copy-start.69 = (f32[1,512]{1,0:T(1,128)S(1)}, f32[1,512]{1,0:T(1,128)}, u32[]{:S(2)}) copy-start(f32[1,512]{1,0:T(1,128)} %get-tuple-element.162) | copy-start | bytes 6148
  169.4 6.3 %copy-start.70 = (f32[1,512]{1,0:T(1,128)S(1)}, f32[1,512]{1,0:T(1,128)}, u32[]{:S(2)}) copy-start(f32[1,512]{1,0:T(1,128)} %get-tuple-element.163) | copy-start | bytes 6148
  169.5 6.8 %copy-start.66 = (f32[1,512,1]{1,0,2:T(1,128)S(1)}, f32[1,512,1]{1,0,2:T(1,128)}, u32[]{:S(2)}) copy-start(f32[1,512,1]{1,0,2:T(1,128)} %fusion.145) | copy-start | bytes 6148
  169.5 7.4 %copy-start.55 = (f32[512]{0:T(512)S(1)}, f32[512]{0:T(512)}, u32[]{:S(2)}) copy-start(f32[512]{0:T(512)} %slice_reduce_fusion) | copy-start | bytes 6148
  169.5 8.0 %copy-start.12 = (bf16[2,128,512]{2,1,0:T(8,128)(2,1)S(1)}, bf16[2,128,512]{2,1,0:T(8,128)(2,1)}, u32[]{:S(2)}) copy-start(bf16[2,128,512]{2,1,0:T(8,128)(2,1)} %copy-done.11) | copy-start | bytes 786436
  169.5 8.0 %copy-start.29 = (bf16[1,128,512]{2,1,0:T(8,128)(2,1)S(1)}, bf16[1,128,512]{2,1,0:T(8,128)(2,1)}, u32[]{:S(2)}) copy-start(bf16[1,128,512]{2,1,0:T(8,128)(2,1)} %copy-done.28) | copy-start | bytes 393220
  (49 other events, 94.3 us)
Sparse Core Ops, SparseCore 0:
  103.3 66.0 all-reduce.53
  172.5 69.1 all-reduce.55
